TPU v7x, 32 devices: a whole 2x2x4 slice. The times are simulated.
32 devices in a mesh: row: 8 (over y, x, core), col: 4 (over z).
Axes of the slice: x: 2, y: 2, z: 4, core: 2. Of those that a mesh axis runs over, the one named last changes fastest.
Arguments:
- row_cells: int32 [3, 8192], P(None, 'row'), may hold values from 0 to 63
- col_cells: int32 [3, 32768], P(None, 'col'), may hold values from 0 to 63
- omega: float32 [16, 32768], P(None, 'col'), may hold values from -6 to 6
Outputs:
- basis: float32 [16, 8192], P(None, 'row')
- image: float32 [16, 32768], P(None, 'col')
- core: float32 [16, 16], replicated
All inputs are finite; a program needn't handle non-finite values.
Results may differ from a plain program's by a relative error of at most 0.0001.
Values sent between devices are 32-bit elements; how exact they have to be, the bound alone decides.
A program may use at most 64 MiB of HBM per device.

v0:
```python
import jax
import jax.numpy as jnp
from jax import lax
from jax.sharding import PartitionSpec as P


def kernel_tile(rows, cols):
    first = (rows[0][:, None] - cols[0][None, :]).astype(jnp.float32)
    total = first * first
    second = (rows[1][:, None] - cols[1][None, :]).astype(jnp.float32)
    total = total + second * second
    third = (rows[2][:, None] - cols[2][None, :]).astype(jnp.float32)
    total = total + third * third
    return 0.25 * jnp.exp(-jnp.sqrt(total) / 6.4)


def shards(row_cells, col_cells, omega):
    rank = omega.shape[0]
    local_rows = row_cells.shape[1]
    local_cols = col_cells.shape[1]
    rows_total = local_rows * lax.axis_size("row")
    order = local_cols * lax.axis_size("col")
    width = min(local_cols, 2048)
    count = local_cols // width

    def tile_at(index):
        cols = lax.dynamic_slice_in_dim(col_cells, index * width, width, 1)
        return kernel_tile(row_cells, cols)

    tiles = lax.map(tile_at, jnp.arange(count, dtype=jnp.int32))
    sketch_part = jnp.einsum(
        "kbw,bmw->km", omega.reshape(rank, count, width), tiles, precision=lax.Precision.HIGHEST
    )
    sketch = lax.psum(sketch_part, "col")
    gram = lax.psum(jnp.dot(sketch, sketch.T, precision=lax.Precision.HIGHEST), "row") / rows_total
    lower = jnp.linalg.cholesky(gram)
    basis = jax.scipy.linalg.solve_triangular(lower, sketch, lower=True)
    image_part = jnp.einsum("km,bmw->kbw", basis, tiles, precision=lax.Precision.HIGHEST).reshape(
        rank, local_cols
    )
    image = lax.psum(image_part, "row")
    core = lax.psum(jnp.dot(image, image.T, precision=lax.Precision.HIGHEST), "col") / order
    return (basis, image, core)


def solution(mesh):
    return jax.shard_map(
        shards,
        mesh=mesh,
        in_specs=(P(None, "row"), P(None, "col"), P(None, "col")),
        out_specs=(P(None, "row"), P(None, "col"), P()),
        check_vma=False,
    )
```

profile of v0, /device:TPU:0, one launch (start us, length us, event | category | flops | bytes accessed | tf_op | source)
XLA Modules:
  0.0 236.3 jit_solution(15518683551914293562)
XLA Ops:
  7.2 43.4 %while.10 = (s32[]{:T(128)}, f32[4,1024,2048]{2,1,0:T(8,128)}, s32[3,1024]{1,0:T(4,128)}, s32[4]{0:T(128)S(1)}, s32[3,8192]{1,0:T(4,128)}, /*index=5*/s32[]{:T(1...) while((s32[]{:T(128)}, f32[4,1024,2048]{2,1,0:T(8,128)}, s32[3,1024]{1,0:T(4,128)}, ...), condition=%wide.region_1.2_spmd, body=%wide.region_0.1_spmd.sunk | while | flops 29360136 | bytes 8499915 | solution.py:30
  7.3 0.6 dynamic_slice.8
  8.5 1.0 constant_dynamic-slice_fusion.2
  9.5 0.8 fusion.18
  10.3 7.8 %multiply_dynamic-update-slice_fusion.2 = f32[4,1024,2048]{2,1,0:T(8,128)} fusion(f32[4,1024,2048]{2,1,0:T(8,128)} %get-tuple-element.102, s32[]{:T(128)} %get-tuple-element.101, s32[2048]{0:T(1024)S(1)} %bitcast.54, s32[1024]{0:T(1024)S(1)} %bitcast.57, s32[2048]{0:T(1024)S(1)} %bitcast.53, s32[1024]{0:T(1024)S(1)} %bitcast.58, s32[2048]{0:T(1024)S(1)} %bitcast.52, ...), kind=kLoop, calls=%fused_computation.clone.1 | loop fusion | flops 29360128 | bytes 8425984 | tf_op jit(solution)/shard_map/while/body/jit(dynamic_update_index_in_dim)/dynamic_update_slice | solution.py:30
  18.1 0.6 dynamic_slice.8
  19.4 1.0 constant_dynamic-slice_fusion.2
  20.3 0.8 fusion.18
  21.2 7.8 %multiply_dynamic-update-slice_fusion.2 = f32[4,1024,2048]{2,1,0:T(8,128)} fusion(f32[4,1024,2048]{2,1,0:T(8,128)} %get-tuple-element.102, s32[]{:T(128)} %get-tuple-element.101, s32[2048]{0:T(1024)S(1)} %bitcast.54, s32[1024]{0:T(1024)S(1)} %bitcast.57, s32[2048]{0:T(1024)S(1)} %bitcast.53, s32[1024]{0:T(1024)S(1)} %bitcast.58, s32[2048]{0:T(1024)S(1)} %bitcast.52, ...), kind=kLoop, calls=%fused_computation.clone.1 | loop fusion | flops 29360128 | bytes 8425984 | tf_op jit(solution)/shard_map/while/body/jit(dynamic_update_index_in_dim)/dynamic_update_slice | solution.py:30
  29.0 0.6 dynamic_slice.8
  30.2 1.0 constant_dynamic-slice_fusion.2
  31.2 0.8 fusion.18
  32.0 7.8 %multiply_dynamic-update-slice_fusion.2 = f32[4,1024,2048]{2,1,0:T(8,128)} fusion(f32[4,1024,2048]{2,1,0:T(8,128)} %get-tuple-element.102, s32[]{:T(128)} %get-tuple-element.101, s32[2048]{0:T(1024)S(1)} %bitcast.54, s32[1024]{0:T(1024)S(1)} %bitcast.57, s32[2048]{0:T(1024)S(1)} %bitcast.53, s32[1024]{0:T(1024)S(1)} %bitcast.58, s32[2048]{0:T(1024)S(1)} %bitcast.52, ...), kind=kLoop, calls=%fused_computation.clone.1 | loop fusion | flops 29360128 | bytes 8425984 | tf_op jit(solution)/shard_map/while/body/jit(dynamic_update_index_in_dim)/dynamic_update_slice | solution.py:30
  41.1 1.0 constant_dynamic-slice_fusion.2
  42.0 0.8 fusion.18
  42.9 7.8 %multiply_dynamic-update-slice_fusion.2 = f32[4,1024,2048]{2,1,0:T(8,128)} fusion(f32[4,1024,2048]{2,1,0:T(8,128)} %get-tuple-element.102, s32[]{:T(128)} %get-tuple-element.101, s32[2048]{0:T(1024)S(1)} %bitcast.54, s32[1024]{0:T(1024)S(1)} %bitcast.57, s32[2048]{0:T(1024)S(1)} %bitcast.53, s32[1024]{0:T(1024)S(1)} %bitcast.58, s32[2048]{0:T(1024)S(1)} %bitcast.52, ...), kind=kLoop, calls=%fused_computation.clone.1 | loop fusion | flops 29360128 | bytes 8425984 | tf_op jit(solution)/shard_map/while/body/jit(dynamic_update_index_in_dim)/dynamic_update_slice | solution.py:30
  50.7 32.5 %convolution_bitcast_fusion.1 = f32[16,1024]{1,0:T(8,128)} fusion(f32[4,1024,2048]{2,1,0:T(8,128)} %get-tuple-element.30, f32[2,4,8,2048]{3,2,1,0:T(8,128)S(1)} %bitcast.55), kind=kOutput, calls=%fused_computation.3 | convolution fusion | flops 1610612736 | bytes 34144256 | tf_op jit(solution)/shard_map/kbw,bmw->km/dot_general | solution.py:31
  83.2 37.1 %all-reduce.3.cloned.1.call-done = f32[16,1024]{1,0:T(8,128)} async-done(((f32[16,1024]{1,0:T(8,128)}), f32[16,1024]{1,0:T(8,128)}) %all-reduce.3.cloned.1.call-update) | async-done | bytes 65552 | tf_op jit(solution)/shard_map/psum | solution.py:34
  120.4 1.1 fusion.8
  121.4 12.3 %psum.29 = f32[16,16]{0,1:T(8,128)S(1)} all-reduce(f32[16,16]{0,1:T(8,128)S(1)} %fusion.8), channel_id=1, replica_groups=mesh['row'=8,'col'=4] {'row'}, use_global_device_ids=true, to_apply=%region_3.4 | all-reduce | flops 256 | bytes 2048 | tf_op jit(solution)/shard_map/psum | solution.py:35
  133.9 1.5 cholesky.16
  135.4 0.6 compare_reduce_fusion
  136.0 0.6 fusion.3
  136.7 1.2 custom-call.7
  137.9 1.1 fusion.4
  139.0 19.6 %convolution_bitcast_fusion = f32[4,2,8,2048]{3,2,1,0:T(8,128)S(1)} fusion(f32[4,1024,2048]{2,1,0:T(8,128)} %get-tuple-element.30, f32[16,1024]{1,0:T(8,128)S(1)} %fusion.4), kind=kOutput, calls=%fused_computation.2 | convolution fusion | flops 1610612736 | bytes 34144256 | tf_op jit(solution)/shard_map/km,bmw->kbw/dot_general | solution.py:38
  158.6 0.8 copy.15
  159.5 53.8 %all-reduce.5.cloned.1.call-done = f32[16,8192]{1,0:T(8,128)} async-done(((f32[16,8192]{1,0:T(8,128)}), f32[16,8192]{1,0:T(8,128)}) %all-reduce.5.cloned.1.call-update) | async-done | bytes 524304 | tf_op jit(solution)/shard_map/psum | solution.py:41
  213.2 1.9 fusion.9
  215.2 11.8 %psum.31 = f32[16,16]{1,0:T(8,128)S(1)} all-reduce(f32[16,16]{1,0:T(8,128)S(1)} %fusion.9), channel_id=1, replica_groups=mesh['row'=8,'col'=4] {'col'}, use_global_device_ids=true, to_apply=%region_7.8 | all-reduce | flops 256 | bytes 2048 | tf_op jit(solution)/shard_map/psum | solution.py:42
  227.0 0.6 broadcast_multiply_fusion
  227.6 1.9 copy.29
  (15 shorter events, 0.8 us)
Async XLA Ops:
  7.2 113.2 %all-reduce.3.cloned.1.call-start = ((), (), s32[]{:S(2)}) async-start(), calls=%async_computation | async-start | bytes 131072 | tf_op jit(solution)/shard_map/psum | solution.py:34
  7.2 43.4 %copy-start = (f32[16,8192]{1,0:T(8,128)S(1)}, f32[16,8192]{1,0:T(8,128)}, u32[]{:S(2)}) copy-start(f32[16,8192]{1,0:T(8,128)} %param.7) | copy-start | bytes 1572868
  83.2 130.0 %all-reduce.5.cloned.1.call-start = ((), (), s32[]{:S(2)}) async-start(), calls=%async_computation.1 | async-start | bytes 1048576 | tf_op jit(solution)/shard_map/psum | solution.py:41
  139.0 19.6 %copy-start.1 = (f32[16,1024]{1,0:T(8,128)}, f32[16,1024]{1,0:T(8,128)S(1)}, u32[]{:S(2)}) copy-start(f32[16,1024]{1,0:T(8,128)S(1)} %fusion.4) | copy-start | bytes 196612
Sparse Core Ops, SparseCore 0:
  83.3 37.0 all-reduce.2
  159.6 53.5 all-reduce.4
where the time goes:
time: 237 us; the launch traced here: 236 us
  waiting for transfers between devices  90.9 us (38%)
  matrix products  56.2 us (24%)
  other arithmetic  35.7 us (15%)
  blocking collectives  24.1 us (10%)
  between operations  14.1 us (6%)
  local copies, waits for them, and re-layouts  12.4 us (5%)
  loops' own time  2.68 us (1%)
    psum x1, waiting for transfers between devices, shards(): image = lax.psum(image_part, 'row')  53.8 us
    psum x1, waiting for transfers between devices, shards(): sketch = lax.psum(sketch_part, 'col')  37.1 us
    dot_general x1, matrix products, shards(): jnp.einsum('kbw,bmw->km', omega.reshape(rank, count, width), tiles, preci...  32.5 us
    dynamic_update_slice x4, other arithmetic, shards(): tiles = lax.map(tile_at, jnp.arange(count, dtype=jnp.int32))  31.1 us
    dot_general x1, matrix products, shards(): jnp.einsum('km,bmw->kbw', basis, tiles, precision=lax.Precision.HIGHEST)  19.6 us
    psum x1, blocking collectives, shards(): lax.psum(jnp.dot(sketch, sketch.T, precision=lax.Precision.HIGHEST), 'row')  12.3 us
    psum x1, blocking collectives, shards(): lax.psum(jnp.dot(image, image.T, precision=lax.Precision.HIGHEST), 'col')  11.8 us
    slice x8, local copies, waits for them, and re-layouts, kernel_tile(): first = (rows[0][:, None] - cols[0][None, :]).astype(jnp.float32)  7.27 us
  transfers between devices with their start and end apart: 2, of which 2 were waited for; matrix products, arithmetic and copies ran while one was open for 0% of the time, Pallas kernels for 0%

commit v1 on v0

--- a/solution.py
+++ b/solution.py
@@ -31,7 +31,7 @@
     sketch_part = jnp.einsum(
         "kbw,bmw->km", omega.reshape(rank, count, width), tiles, precision=lax.Precision.HIGHEST
     )
-    sketch = lax.psum(sketch_part, "col")
+    sketch = jnp.sum(lax.all_gather(sketch_part, "col"), axis=0)
     gram = lax.psum(jnp.dot(sketch, sketch.T, precision=lax.Precision.HIGHEST), "row") / rows_total
     lower = jnp.linalg.cholesky(gram)
     basis = jax.scipy.linalg.solve_triangular(lower, sketch, lower=True)

time: 237 us -> 213 us (0.90)
  waiting for transfers between devices: 90.9 us -> 55.5 us
  blocking collectives: 24.1 us -> 39.9 us
  matrix products: 56.2 us -> 51.8 us
    psum x1 -> x0, waiting for transfers between devices: 37.1 us -> none  [shards(): sketch = lax.psum(sketch_part, 'col')]
    all_gather x0 -> x1, blocking collectives: none -> 15.7 us  [shards(): sketch = jnp.sum(lax.all_gather(sketch_part, 'col'), axis=0)]
    dot_general x1, matrix products: 32.5 us -> 29.8 us  [shards(): jnp.einsum('kbw,bmw->km', omega.reshape(rank, count, width), tiles, preci...]
  transfers between devices with their start and end apart: 2 -> 1, of which waited for: 2 -> 1; matrix products, arithmetic and copies ran while one was open for 0% -> 0% of each run, Pallas kernels for 0% -> 0%
where the time goes in v1:
time: 213 us; the launch traced here: 212 us
  waiting for transfers between devices  55.5 us (26%)
  matrix products  51.8 us (24%)
  blocking collectives  39.9 us (19%)
  other arithmetic  35.8 us (17%)
  between operations  14.1 us (7%)
  local copies, waits for them, and re-layouts  12.4 us (6%)
  loops' own time  2.68 us (1%)
    psum x1, waiting for transfers between devices, shards(): image = lax.psum(image_part, 'row')  55.5 us
    dynamic_update_slice x4, other arithmetic, shards(): tiles = lax.map(tile_at, jnp.arange(count, dtype=jnp.int32))  31.1 us
    dot_general x1, matrix products, shards(): jnp.einsum('kbw,bmw->km', omega.reshape(rank, count, width), tiles, preci...  29.8 us
    dot_general x1, matrix products, shards(): jnp.einsum('km,bmw->kbw', basis, tiles, precision=lax.Precision.HIGHEST)  19.6 us
    all_gather x1, blocking collectives, shards(): sketch = jnp.sum(lax.all_gather(sketch_part, 'col'), axis=0)  15.7 us
    psum x1, blocking collectives, shards(): lax.psum(jnp.dot(sketch, sketch.T, precision=lax.Precision.HIGHEST), 'row')  12.4 us
    psum x1, blocking collectives, shards(): lax.psum(jnp.dot(image, image.T, precision=lax.Precision.HIGHEST), 'col')  11.8 us
    slice x8, local copies, waits for them, and re-layouts, kernel_tile(): first = (rows[0][:, None] - cols[0][None, :]).astype(jnp.float32)  7.27 us
  transfers between devices with their start and end apart: 1, of which 1 were waited for; matrix products, arithmetic and copies ran while one was open for 0% of the time, Pallas kernels for 0%

profile of v1, /device:TPU:0, one launch (start us, length us, event | category | flops | bytes accessed | tf_op | source)
XLA Modules:
  0.0 212.2 jit_solution(17949065155297085237)
XLA Ops:
  7.2 43.4 %while.10 = (s32[]{:T(128)}, f32[4,1024,2048]{2,1,0:T(8,128)}, s32[3,1024]{1,0:T(4,128)}, s32[4]{0:T(128)S(1)}, s32[3,8192]{1,0:T(4,128)}, /*index=5*/s32[]{:T(1...) while((s32[]{:T(128)}, f32[4,1024,2048]{2,1,0:T(8,128)}, s32[3,1024]{1,0:T(4,128)}, ...), condition=%wide.region_1.2_spmd, body=%wide.region_0.1_spmd.sunk | while | flops 29360136 | bytes 8499915 | solution.py:30
  7.3 0.6 dynamic_slice.8
  8.5 1.0 constant_dynamic-slice_fusion.2
  9.5 0.8 fusion.18
  10.3 7.8 %multiply_dynamic-update-slice_fusion.2 = f32[4,1024,2048]{2,1,0:T(8,128)} fusion(f32[4,1024,2048]{2,1,0:T(8,128)} %get-tuple-element.102, s32[]{:T(128)} %get-tuple-element.101, s32[2048]{0:T(1024)S(1)} %bitcast.56, s32[1024]{0:T(1024)S(1)} %bitcast.59, s32[2048]{0:T(1024)S(1)} %bitcast.55, s32[1024]{0:T(1024)S(1)} %bitcast.60, s32[2048]{0:T(1024)S(1)} %bitcast.54, ...), kind=kLoop, calls=%fused_computation.clone.1 | loop fusion | flops 29360128 | bytes 8425984 | tf_op jit(solution)/shard_map/while/body/jit(dynamic_update_index_in_dim)/dynamic_update_slice | solution.py:30
  18.1 0.6 dynamic_slice.8
  19.4 1.0 constant_dynamic-slice_fusion.2
  20.3 0.8 fusion.18
  21.2 7.8 %multiply_dynamic-update-slice_fusion.2 = f32[4,1024,2048]{2,1,0:T(8,128)} fusion(f32[4,1024,2048]{2,1,0:T(8,128)} %get-tuple-element.102, s32[]{:T(128)} %get-tuple-element.101, s32[2048]{0:T(1024)S(1)} %bitcast.56, s32[1024]{0:T(1024)S(1)} %bitcast.59, s32[2048]{0:T(1024)S(1)} %bitcast.55, s32[1024]{0:T(1024)S(1)} %bitcast.60, s32[2048]{0:T(1024)S(1)} %bitcast.54, ...), kind=kLoop, calls=%fused_computation.clone.1 | loop fusion | flops 29360128 | bytes 8425984 | tf_op jit(solution)/shard_map/while/body/jit(dynamic_update_index_in_dim)/dynamic_update_slice | solution.py:30
  29.0 0.6 dynamic_slice.8
  30.2 1.0 constant_dynamic-slice_fusion.2
  31.2 0.8 fusion.18
  32.0 7.8 %multiply_dynamic-update-slice_fusion.2 = f32[4,1024,2048]{2,1,0:T(8,128)} fusion(f32[4,1024,2048]{2,1,0:T(8,128)} %get-tuple-element.102, s32[]{:T(128)} %get-tuple-element.101, s32[2048]{0:T(1024)S(1)} %bitcast.56, s32[1024]{0:T(1024)S(1)} %bitcast.59, s32[2048]{0:T(1024)S(1)} %bitcast.55, s32[1024]{0:T(1024)S(1)} %bitcast.60, s32[2048]{0:T(1024)S(1)} %bitcast.54, ...), kind=kLoop, calls=%fused_computation.clone.1 | loop fusion | flops 29360128 | bytes 8425984 | tf_op jit(solution)/shard_map/while/body/jit(dynamic_update_index_in_dim)/dynamic_update_slice | solution.py:30
  39.8 0.6 dynamic_slice.8
  41.1 1.0 constant_dynamic-slice_fusion.2
  42.0 0.8 fusion.18
  42.9 7.8 %multiply_dynamic-update-slice_fusion.2 = f32[4,1024,2048]{2,1,0:T(8,128)} fusion(f32[4,1024,2048]{2,1,0:T(8,128)} %get-tuple-element.102, s32[]{:T(128)} %get-tuple-element.101, s32[2048]{0:T(1024)S(1)} %bitcast.56, s32[1024]{0:T(1024)S(1)} %bitcast.59, s32[2048]{0:T(1024)S(1)} %bitcast.55, s32[1024]{0:T(1024)S(1)} %bitcast.60, s32[2048]{0:T(1024)S(1)} %bitcast.54, ...), kind=kLoop, calls=%fused_computation.clone.1 | loop fusion | flops 29360128 | bytes 8425984 | tf_op jit(solution)/shard_map/while/body/jit(dynamic_update_index_in_dim)/dynamic_update_slice | solution.py:30
  50.7 29.8 %convolution_bitcast_fusion.1 = f32[16,1024]{1,0:T(8,128)S(1)} fusion(f32[4,1024,2048]{2,1,0:T(8,128)} %get-tuple-element.30, f32[2,4,8,2048]{3,2,1,0:T(8,128)S(1)} %bitcast.57), kind=kOutput, calls=%fused_computation.3 | convolution fusion | flops 1610612736 | bytes 34144256 | tf_op jit(solution)/shard_map/kbw,bmw->km/dot_general | solution.py:31
  80.5 15.7 %all-gather = f32[64,1024]{1,0:T(8,128)S(1)} all-gather(f32[16,1024]{1,0:T(8,128)S(1)} %convolution_bitcast_fusion.1), channel_id=2, replica_groups=mesh['row'=8,'col'=4] {'col'}, dimensions={0}, use_global_device_ids=true | all-gather | bytes 327680 | tf_op jit(solution)/shard_map/all_gather | solution.py:34
  96.3 12.4 %psum.21 = f32[16,16]{0,1:T(8,128)S(1)} all-reduce(f32[16,16]{0,1:T(8,128)S(1)} %fusion.8), channel_id=1, replica_groups=mesh['row'=8,'col'=4] {'row'}, use_global_device_ids=true, to_apply=%region_3.4 | all-reduce | flops 256 | bytes 2048 | tf_op jit(solution)/shard_map/psum | solution.py:35
  108.9 1.5 cholesky.16
  110.4 0.6 compare_reduce_fusion
  111.0 0.6 fusion.3
  111.7 1.2 custom-call.7
  112.9 0.3 fusion.4
  113.2 19.6 %convolution_bitcast_fusion = f32[4,2,8,2048]{3,2,1,0:T(8,128)S(1)} fusion(f32[4,1024,2048]{2,1,0:T(8,128)} %get-tuple-element.30, f32[16,1024]{1,0:T(8,128)S(1)} %fusion.4), kind=kOutput, calls=%fused_computation.2 | convolution fusion | flops 1610612736 | bytes 34144256 | tf_op jit(solution)/shard_map/km,bmw->kbw/dot_general | solution.py:38
  132.8 0.8 copy.15
  133.6 55.5 %all-reduce.2.cloned.1.call-done = f32[16,8192]{1,0:T(8,128)} async-done(((f32[16,8192]{1,0:T(8,128)}), f32[16,8192]{1,0:T(8,128)}) %all-reduce.2.cloned.1.call-update) | async-done | bytes 524304 | tf_op jit(solution)/shard_map/psum | solution.py:41
  189.1 1.9 fusion.9
  191.1 11.8 %psum.23 = f32[16,16]{1,0:T(8,128)S(1)} all-reduce(f32[16,16]{1,0:T(8,128)S(1)} %fusion.9), channel_id=1, replica_groups=mesh['row'=8,'col'=4] {'col'}, use_global_device_ids=true, to_apply=%region_7.8 | all-reduce | flops 256 | bytes 2048 | tf_op jit(solution)/shard_map/psum | solution.py:42
  202.8 0.6 broadcast_multiply_fusion
  203.4 1.9 copy.28
  (14 shorter events, 0.4 us)
Async XLA Ops:
  7.2 182.0 %all-reduce.2.cloned.1.call-start = ((), (), s32[]{:S(2)}) async-start(), calls=%async_computation | async-start | bytes 1048576 | tf_op jit(solution)/shard_map/psum | solution.py:41
  7.2 43.4 %copy-start = (f32[16,8192]{1,0:T(8,128)S(1)}, f32[16,8192]{1,0:T(8,128)}, u32[]{:S(2)}) copy-start(f32[16,8192]{1,0:T(8,128)} %param.7) | copy-start | bytes 1572868
  113.2 19.6 %copy-start.1 = (f32[16,1024]{1,0:T(8,128)}, f32[16,1024]{1,0:T(8,128)S(1)}, u32[]{:S(2)}) copy-start(f32[16,1024]{1,0:T(8,128)S(1)} %fusion.4) | copy-start | bytes 196612
Sparse Core Ops, SparseCore 0:
  133.8 55.3 all-reduce.1
